TPU v7x, 32 devices: a whole 2x2x4 slice. The times are simulated.
32 devices in a mesh: shot: 4 (over y, core), tile: 8 (over z, x).
Axes of the slice: x: 2, y: 2, z: 4, core: 2. Of those that a mesh axis runs over, the one named last changes fastest.
Arguments:
- source: bfloat16 [64, 1, 32, 32, 128], P(('shot', 'tile')), may hold values from -6 to 6
- receiver: bfloat16 [64, 1, 32, 32, 128], P(('shot', 'tile')), may hold values from -6 to 6
- corners: int32 [64, 2], P(('shot', 'tile')), may hold values from 0 to 224, as said below
Outputs:
- filtered: float32 [32, 256, 256], P('tile', 'shot')
Inputs may be any that keep to these rules, and one draw needn't show every extreme that they name: corners[s, 0] is at most 224 and corners[s, 1] at most 128, so every box lies inside the image.
All inputs are finite; a program needn't handle non-finite values.
Results may differ from a plain program's by a relative error of at most 0.0003.
Values may be sent and summed in bfloat16 or wider, within the bound.
A program may use at most 64 MiB of HBM per device.

v0:
```python
import jax
import jax.numpy as jnp
from jax import lax
from jax.sharding import PartitionSpec as P

X = 256
Y = 256
damping = 1.0


def with_halo(cells, sides, width):
    for axis, dim in sides:
        count = lax.axis_size(axis)
        ends = count - 1
        head = lax.slice_in_dim(cells, 0, width, axis=dim)
        tail = lax.slice_in_dim(cells, cells.shape[dim] - width, cells.shape[dim], axis=dim)
        cells = jnp.concatenate(
            [
                lax.ppermute(tail, axis, [(i, (i + 1) % count) for i in range(ends)]),
                cells,
                lax.ppermute(head, axis, [((i + 1) % count, i) for i in range(ends)]),
            ],
            axis=dim,
        )
    return cells


def laplace(padded):
    center = padded[1:-1, 1:-1, 1:-1]
    beside = padded[2:, 1:-1, 1:-1] + padded[:-2, 1:-1, 1:-1]
    beside = beside + padded[1:-1, 2:, 1:-1] + padded[1:-1, :-2, 1:-1]
    beside = beside + padded[1:-1, 1:-1, 2:] + padded[1:-1, 1:-1, :-2]
    return beside - 6.0 * center


def correlate(wave_bf, back_bf, time_axis):
    wave = wave_bf.astype(jnp.float32)
    back = back_bf.astype(jnp.float32)
    return jnp.stack((jnp.sum(wave * back, axis=time_axis), jnp.sum(wave * wave, axis=time_axis)))


def per_device(source, receiver, corners):
    tile_count = lax.axis_size("tile")
    slab_depth = source.shape[2] // tile_count
    box_rows = source.shape[3]
    box_cols = source.shape[4]
    got_wave, got_back = (
        lax.all_to_all(source, "tile", split_axis=2, concat_axis=0, tiled=True),
        lax.all_to_all(receiver, "tile", split_axis=2, concat_axis=0, tiled=True),
    )
    stacked = correlate(got_wave, got_back, 1)
    corner_all = lax.all_gather(corners, "tile", axis=0, tiled=True)
    col_index = jnp.arange(Y, dtype=jnp.int32)
    box_col = jnp.arange(box_cols, dtype=jnp.int32)
    col_table = (
        col_index[None, None, :] == corner_all[:, 1][:, None, None] + box_col[None, :, None]
    ).astype(jnp.float32)
    placed = jnp.einsum("qkzab,kby->qzkay", stacked, col_table, precision=lax.Precision.HIGHEST)
    shots_in = corner_all.shape[0]
    placed = placed.reshape(2, slab_depth, shots_in * box_rows, Y)
    row_target = (
        corner_all[:, 0][:, None] + jnp.arange(box_rows, dtype=jnp.int32)[None, :]
    ).reshape(-1)
    row_index = jnp.arange(X, dtype=jnp.int32)
    row_table = (row_target[:, None] == row_index[None, :]).astype(jnp.float32)
    sums = jnp.einsum("rx,qzry->qzxy", row_table, placed, precision=lax.Precision.HIGHEST)
    image_part = sums[0]
    light_part = sums[1]
    image_sum, light_sum = (
        lax.psum_scatter(image_part, "shot", scatter_dimension=1, tiled=True),
        lax.psum_scatter(light_part, "shot", scatter_dimension=1, tiled=True),
    )
    normal = image_sum / (damping + light_sum)
    padded = with_halo(normal, (("shot", 1), ("tile", 0)), 1)
    padded = jnp.pad(padded, ((0, 0), (0, 0), (1, 1)))
    return laplace(padded)


def solution(mesh):
    return jax.shard_map(
        per_device,
        mesh=mesh,
        in_specs=(
            P(("shot", "tile"), None, None, None, None),
            P(("shot", "tile"), None, None, None, None),
            P(("shot", "tile"), None),
        ),
        out_specs=P("tile", "shot", None),
        check_vma=False,
    )
```

profile of v0, /device:TPU:3, one launch (start us, length us, event | category | flops | bytes accessed | tf_op | source)
XLA Modules:
  0.0 143.1 jit_solution(10602599561009317554)
XLA Ops:
  6.5 2.0 %copy.15 = bf16[2,1,32,32,128]{4,3,1,0,2:T(8,128)(2,1)} copy(bf16[2,1,32,32,128]{4,3,2,1,0:T(8,128)(2,1)} %param.3) | data formatting | bytes 1048576 | tf_op args[0]
  8.5 5.8 %all-to-all-start = ((bf16[2,1,32,32,128]{4,3,1,0,2:T(8,128)(2,1)}), bf16[2,1,32,32,128]{4,3,1,0,2:T(8,128)(2,1)S(1)}, u32[]{:S(2)}, u32[]{:S(2)}) async-start(bf16[2,1,32,32,128]{4,3,1,0,2:T(8,128)(2,1)} %copy.15), calls=%async_computation | async-start | bytes 1048576 | tf_op jit(solution)/shard_map/all_to_all | solution.py:48
  14.3 0.9 copy.16
  15.2 12.9 %all-to-all-done = bf16[2,1,32,32,128]{4,3,1,0,2:T(8,128)(2,1)S(1)} async-done(((bf16[2,1,32,32,128]{4,3,1,0,2:T(8,128)(2,1)}), bf16[2,1,32,32,128]{4,3,1,0,2:T(8,128)(2,1)S(1)}, u32[]{:S(2)}, u32[]{:S(2)}) %all-to-all-start) | async-done | bytes 524320 | tf_op jit(solution)/shard_map/all_to_all | solution.py:48
  28.1 4.5 %all-to-all-start.1 = ((bf16[2,1,32,32,128]{4,3,1,0,2:T(8,128)(2,1)}), bf16[2,1,32,32,128]{4,3,1,0,2:T(8,128)(2,1)S(1)}, u32[]{:S(2)}, u32[]{:S(2)}) async-start(bf16[2,1,32,32,128]{4,3,1,0,2:T(8,128)(2,1)} %copy.16), calls=%async_computation.1 | async-start | bytes 1048576 | tf_op jit(solution)/shard_map/all_to_all | solution.py:49
  32.6 19.9 %all-gather = s32[8,2,2]{2,1,0:T(2,128)S(1)} all-gather(s32[1,2,2]{2,1,0:T(2,128)S(1)} %bitcast.41), channel_id=1, replica_groups=mesh['shot'=4,'tile'=8] {'tile'}, dimensions={0}, use_global_device_ids=true | all-gather | bytes 144 | tf_op jit(solution)/shard_map/all_gather | solution.py:52
  53.0 0.3 convert_multiply_fusion.1
  53.4 2.3 %convolution_bitcast_fusion = f32[2,4,16,32,256]{4,3,1,0,2:T(8,128)S(1)} fusion(f32[1,16,4,32,128]{4,3,2,0,1:T(8,128)S(1)} %bitcast.37, f32[1,16,4,32,128]{4,3,2,0,1:T(8,128)S(1)} %bitcast.36, s32[16,128]{1,0:T(8,128)S(1)} %iota_add_fusion.1), kind=kOutput, calls=%fused_computation | convolution fusion | flops 1611661312 | bytes 6299648 | tf_op jit(solution)/shard_map/qkzab,kby->qzkay/dot_general | solution.py:58
  55.7 0.6 copy.19
  56.3 3.6 %convolution_bitcast_fusion.1 = f32[2,4,256,256]{2,3,1,0:T(8,128)S(1)} fusion(f32[2,4,512,256]{3,2,1,0:T(8,128)S(1)} %bitcast.33, s32[512]{0:T(512)S(1)} %add.74), kind=kOutput, calls=%fused_computation.6 | convolution fusion | flops 3221356544 | bytes 6293504 | tf_op jit(solution)/shard_map/rx,qzry->qzxy/dot_general | solution.py:66
  60.2 1.3 copy.21
  61.5 1.3 copy.22
  62.9 0.6 dynamic-slice
  64.1 51.9 %all-reduce.6.cloned.1.call-done = (f32[4,256,256]{2,0,1:T(4,128)}, f32[4,256,256]{2,0,1:T(4,128)}) async-done(((f32[4,256,256]{2,0,1:T(4,128)}, f32[4,256,256]{2,0,1:T(4,128)}), (f32[4,256,256]{2,0,1:T(4,128)}, f32[4,256,256]{2,0,1:T(4,128)})) %all-reduce.6.cloned.1.call-update) | async-done | bytes 2097168
  116.0 1.1 fusion.13
  117.1 3.1 %collective-permute-start = (f32[4,1,256]{2,0,1:T(4,128)S(1)}, f32[4,1,256]{2,0,1:T(4,128)S(1)}, u32[]{:S(2)}, u32[]{:S(2)}) collective-permute-start(f32[4,1,256]{2,0,1:T(4,128)S(1)} %get-tuple-element.13), channel_id=1, source_target_pairs={{0,8},{8,16},{16,24},{1,9},{9,17},{17,25},{2,10},{10,18},{18,26},{... | collective-permute-start | bytes 12296 | tf_op jit(solution)/shard_map/ppermute | solution.py:19
  120.2 1.9 %collective-permute-start.1 = (f32[4,1,256]{2,0,1:T(4,128)S(1)}, f32[4,1,256]{2,0,1:T(4,128)S(1)}, u32[]{:S(2)}, u32[]{:S(2)}) collective-permute-start(f32[4,1,256]{2,0,1:T(4,128)S(1)} %get-tuple-element.14), channel_id=1, source_target_pairs={{8,0},{16,8},{24,16},{9,1},{17,9},{25,17},{10,2},{18,10},{26,18},{... | collective-permute-start | bytes 12296 | tf_op jit(solution)/shard_map/ppermute | solution.py:21
  122.1 3.0 %collective-permute-done.1 = f32[4,1,256]{2,0,1:T(4,128)S(1)} collective-permute-done((f32[4,1,256]{2,0,1:T(4,128)S(1)}, f32[4,1,256]{2,0,1:T(4,128)S(1)}, u32[]{:S(2)}, u32[]{:S(2)}) %collective-permute-start.1) | collective-permute-done | bytes 4128 | tf_op jit(solution)/shard_map/ppermute | solution.py:21
  125.2 3.1 %collective-permute-start.3 = (f32[1,66,256]{2,0,1:T(1,128)S(1)}, f32[1,66,256]{2,0,1:T(1,128)S(1)}, u32[]{:S(2)}, u32[]{:S(2)}) collective-permute-start(f32[1,66,256]{2,0,1:T(1,128)S(1)} %get-tuple-element.11), channel_id=1, source_target_pairs={{0,1},{1,2},{2,3},{3,4},{4,5},{5,6},{6,7},{8,9},{9,10},{10,11},{11... | collective-permute-start | bytes 202760 | tf_op jit(solution)/shard_map/ppermute | solution.py:19
  128.3 2.2 %collective-permute-start.2 = (f32[1,66,256]{2,0,1:T(1,128)S(1)}, f32[1,66,256]{2,0,1:T(1,128)S(1)}, u32[]{:S(2)}, u32[]{:S(2)}) collective-permute-start(f32[1,66,256]{2,0,1:T(1,128)S(1)} %get-tuple-element.12), channel_id=1, source_target_pairs={{1,0},{2,1},{3,2},{4,3},{5,4},{6,5},{7,6},{9,8},{10,9},{11,10},{12... | collective-permute-start | bytes 202760 | tf_op jit(solution)/shard_map/ppermute | solution.py:21
  130.5 3.7 %collective-permute-done.2 = f32[1,66,256]{2,0,1:T(1,128)S(1)} collective-permute-done((f32[1,66,256]{2,0,1:T(1,128)S(1)}, f32[1,66,256]{2,0,1:T(1,128)S(1)}, u32[]{:S(2)}, u32[]{:S(2)}) %collective-permute-start.2) | collective-permute-done | bytes 67616 | tf_op jit(solution)/shard_map/ppermute | solution.py:21
  134.3 0.7 select_maximum_fusion
  135.0 0.5 fusion.9
  135.5 0.8 copy.23
  (22 shorter events, 1.0 us)
Async XLA Ops:
  6.5 7.8 %copy-start = (bf16[2,1,32,32,128]{4,3,2,1,0:T(8,128)(2,1)S(1)}, bf16[2,1,32,32,128]{4,3,2,1,0:T(8,128)(2,1)}, u32[]{:S(2)}) copy-start(bf16[2,1,32,32,128]{4,3,2,1,0:T(8,128)(2,1)} %param.4) | copy-start | bytes 1572868
  6.5 26.1 %copy-start.1 = (s32[2,2]{1,0:T(2,128)S(1)}, s32[2,2]{1,0:T(2,128)}, u32[]{:S(2)}) copy-start(s32[2,2]{1,0:T(2,128)} %param.5) | copy-start | bytes 52
  8.5 19.5 %all-to-all-start = ((bf16[2,1,32,32,128]{4,3,1,0,2:T(8,128)(2,1)}), bf16[2,1,32,32,128]{4,3,1,0,2:T(8,128)(2,1)S(1)}, u32[]{:S(2)}, u32[]{:S(2)}) async-start(bf16[2,1,32,32,128]{4,3,1,0,2:T(8,128)(2,1)} %copy.15), calls=%async_computation | async-start | bytes 1048576 | tf_op jit(solution)/shard_map/all_to_all | solution.py:48
  28.1 24.9 %all-to-all-start.1 = ((bf16[2,1,32,32,128]{4,3,1,0,2:T(8,128)(2,1)}), bf16[2,1,32,32,128]{4,3,1,0,2:T(8,128)(2,1)S(1)}, u32[]{:S(2)}, u32[]{:S(2)}) async-start(bf16[2,1,32,32,128]{4,3,1,0,2:T(8,128)(2,1)} %copy.16), calls=%async_computation.1 | async-start | bytes 1048576 | tf_op jit(solution)/shard_map/all_to_all | solution.py:49
  32.6 83.4 %all-reduce.6.cloned.1.call-start = ((), (), s32[]{:S(2)}) async-start(), calls=%async_computation.2 | async-start | bytes 4194304
  61.5 1.3 copy-start.2
  117.1 5.0 %collective-permute-start = (f32[4,1,256]{2,0,1:T(4,128)S(1)}, f32[4,1,256]{2,0,1:T(4,128)S(1)}, u32[]{:S(2)}, u32[]{:S(2)}) collective-permute-start(f32[4,1,256]{2,0,1:T(4,128)S(1)} %get-tuple-element.13), channel_id=1, source_target_pairs={{0,8},{8,16},{16,24},{1,9},{9,17},{17,25},{2,10},{10,18},{18,26},{... | collective-permute-start | bytes 12296 | tf_op jit(solution)/shard_map/ppermute | solution.py:19
  120.2 4.9 %collective-permute-start.1 = (f32[4,1,256]{2,0,1:T(4,128)S(1)}, f32[4,1,256]{2,0,1:T(4,128)S(1)}, u32[]{:S(2)}, u32[]{:S(2)}) collective-permute-start(f32[4,1,256]{2,0,1:T(4,128)S(1)} %get-tuple-element.14), channel_id=1, source_target_pairs={{8,0},{16,8},{24,16},{9,1},{17,9},{25,17},{10,2},{18,10},{26,18},{... | collective-permute-start | bytes 12296 | tf_op jit(solution)/shard_map/ppermute | solution.py:21
  125.2 5.3 %collective-permute-start.3 = (f32[1,66,256]{2,0,1:T(1,128)S(1)}, f32[1,66,256]{2,0,1:T(1,128)S(1)}, u32[]{:S(2)}, u32[]{:S(2)}) collective-permute-start(f32[1,66,256]{2,0,1:T(1,128)S(1)} %get-tuple-element.11), channel_id=1, source_target_pairs={{0,1},{1,2},{2,3},{3,4},{4,5},{5,6},{6,7},{8,9},{9,10},{10,11},{11... | collective-permute-start | bytes 202760 | tf_op jit(solution)/shard_map/ppermute | solution.py:19
  128.3 5.9 %collective-permute-start.2 = (f32[1,66,256]{2,0,1:T(1,128)S(1)}, f32[1,66,256]{2,0,1:T(1,128)S(1)}, u32[]{:S(2)}, u32[]{:S(2)}) collective-permute-start(f32[1,66,256]{2,0,1:T(1,128)S(1)} %get-tuple-element.12), channel_id=1, source_target_pairs={{1,0},{2,1},{3,2},{4,3},{5,4},{6,5},{7,6},{9,8},{10,9},{11,10},{12... | collective-permute-start | bytes 202760 | tf_op jit(solution)/shard_map/ppermute | solution.py:21
Sparse Core Ops, SparseCore 0:
  63.0 52.9 all-reduce.5
where the time goes:
time: 143 us
  waiting for transfers between devices  71.5 us (50%)
  starting transfers between devices  20.6 us (14%)
  blocking collectives  19.9 us (14%)
  between operations  14.2 us (10%)
  local copies, waits for them, and re-layouts  8.1 us (6%)
  matrix products  5.91 us (4%)
  other arithmetic  2.88 us (2%)
    unnamed x2, waiting for transfers between devices  51.9 us
    all_gather x1, blocking collectives, per_device(): corner_all = lax.all_gather(corners, 'tile', axis=0, tiled=True)  19.9 us
    all_to_all x1, waiting for transfers between devices, per_device(): lax.all_to_all(source, 'tile', split_axis=2, concat_axis=0, tiled=True)  12.9 us
    ppermute x2, waiting for transfers between devices, with_halo(): lax.ppermute(head, axis, [((i + 1) % count, i) for i in range(ends)])  6.73 us
    ppermute x2, starting transfers between devices, with_halo(): lax.ppermute(tail, axis, [(i, (i + 1) % count) for i in range(ends)])  6.16 us
    all_to_all x1, starting transfers between devices, per_device(): lax.all_to_all(source, 'tile', split_axis=2, concat_axis=0, tiled=True)  5.78 us
    all_to_all x1, starting transfers between devices, per_device(): lax.all_to_all(receiver, 'tile', split_axis=2, concat_axis=0, tiled=True)  4.54 us
    ppermute x2, starting transfers between devices, with_halo(): lax.ppermute(head, axis, [((i + 1) % count, i) for i in range(ends)])  4.09 us
  transfers between devices with their start and end apart: 7, of which 4 were waited for; matrix products, arithmetic and copies ran while one was open for 1% of the time, Pallas kernels for 0%

commit v1 on v0

--- a/solution.py
+++ b/solution.py
@@ -49,7 +49,15 @@
         lax.all_to_all(receiver, "tile", split_axis=2, concat_axis=0, tiled=True),
     )
     stacked = correlate(got_wave, got_back, 1)
-    corner_all = lax.all_gather(corners, "tile", axis=0, tiled=True)
+    ways, here, step = (lax.axis_size("tile"), lax.axis_index("tile"), corners.shape[0])
+    line, have = (corners, 1)
+    while have < ways:
+        line = jnp.concatenate(
+            [line, lax.ppermute(line, "tile", [(d, (d - have) % ways) for d in range(ways)])],
+            axis=0,
+        )
+        have = 2 * have
+    corner_all = jnp.roll(line, here * step, axis=0)
     col_index = jnp.arange(Y, dtype=jnp.int32)
     box_col = jnp.arange(box_cols, dtype=jnp.int32)
     col_table = (

time: 143 us -> 139 us (0.972); the launches traced: 143 us -> 137 us
  blocking collectives: 19.9 us -> 0 us
  starting transfers between devices: 20.6 us -> 29.5 us
  waiting for transfers between devices: 71.5 us -> 76.2 us
    all_gather x1 -> x0, blocking collectives: 19.9 us -> none  [per_device(): corner_all = lax.all_gather(corners, 'tile', axis=0, tiled=True)]
    ppermute x0 -> x3, starting transfers between devices: none -> 8.06 us  [per_device(): lax.ppermute(line, 'tile', [(d, (d - have) % ways) for d in range(ways)])]
    ppermute x0 -> x3, waiting for transfers between devices: none -> 6.27 us  [per_device(): lax.ppermute(line, 'tile', [(d, (d - have) % ways) for d in range(ways)])]
    ppermute x2, waiting for transfers between devices: 6.73 us -> 2.99 us  [with_halo(): lax.ppermute(head, axis, [((i + 1) % count, i) for i in range(ends)])]
    unnamed x11 -> x10, local copies, waits for them, and re-layouts: 3.6 us -> 3.52 us
  transfers between devices with their start and end apart: 7 -> 10, of which waited for: 4 -> 6; matrix products, arithmetic and copies ran while one was open for 1% -> 2% of each run, Pallas kernels for 0% -> 0%
where the time goes in v1:
time: 139 us; the launch traced here: 137 us
  waiting for transfers between devices  76.2 us (55%)
  starting transfers between devices  29.5 us (21%)
  between operations  14.2 us (10%)
  local copies, waits for them, and re-layouts  8.1 us (6%)
  matrix products  5.9 us (4%)
  other arithmetic  3.03 us (2%)
    unnamed x2, waiting for transfers between devices  52.9 us
    all_to_all x1, waiting for transfers between devices, per_device(): lax.all_to_all(source, 'tile', split_axis=2, concat_axis=0, tiled=True)  12.8 us
    ppermute x3, starting transfers between devices, per_device(): lax.ppermute(line, 'tile', [(d, (d - have) % ways) for d in range(ways)])  8.06 us
    ppermute x2, starting transfers between devices, with_halo(): lax.ppermute(tail, axis, [(i, (i + 1) % count) for i in range(ends)])  7.25 us
    ppermute x3, waiting for transfers between devices, per_device(): lax.ppermute(line, 'tile', [(d, (d - have) % ways) for d in range(ways)])  6.27 us
    all_to_all x1, starting transfers between devices, per_device(): lax.all_to_all(source, 'tile', split_axis=2, concat_axis=0, tiled=True)  5.78 us
    all_to_all x1, starting transfers between devices, per_device(): lax.all_to_all(receiver, 'tile', split_axis=2, concat_axis=0, tiled=True)  4.54 us
    ppermute x2, starting transfers between devices, with_halo(): lax.ppermute(head, axis, [((i + 1) % count, i) for i in range(ends)])  3.9 us
  transfers between devices with their start and end apart: 10, of which 6 were waited for; matrix products, arithmetic and copies ran while one was open for 2% of the time, Pallas kernels for 0%

profile of v1, /device:TPU:3, one launch (start us, length us, event | category | flops | bytes accessed | tf_op | source)
XLA Modules:
  0.0 137.0 jit_solution(15454894999807488901)
XLA Ops:
  6.5 2.0 %copy.17 = bf16[2,1,32,32,128]{4,3,1,0,2:T(8,128)(2,1)} copy(bf16[2,1,32,32,128]{4,3,2,1,0:T(8,128)(2,1)} %param.3) | data formatting | bytes 1048576 | tf_op args[0]
  8.5 5.8 %all-to-all-start = ((bf16[2,1,32,32,128]{4,3,1,0,2:T(8,128)(2,1)}), bf16[2,1,32,32,128]{4,3,1,0,2:T(8,128)(2,1)S(1)}, u32[]{:S(2)}, u32[]{:S(2)}) async-start(bf16[2,1,32,32,128]{4,3,1,0,2:T(8,128)(2,1)} %copy.17), calls=%async_computation | async-start | bytes 1048576 | tf_op jit(solution)/shard_map/all_to_all | solution.py:48
  14.4 0.9 copy.18
  15.3 12.8 %all-to-all-done = bf16[2,1,32,32,128]{4,3,1,0,2:T(8,128)(2,1)S(1)} async-done(((bf16[2,1,32,32,128]{4,3,1,0,2:T(8,128)(2,1)}), bf16[2,1,32,32,128]{4,3,1,0,2:T(8,128)(2,1)S(1)}, u32[]{:S(2)}, u32[]{:S(2)}) %all-to-all-start) | async-done | bytes 524320 | tf_op jit(solution)/shard_map/all_to_all | solution.py:48
  28.1 4.5 %all-to-all-start.1 = ((bf16[2,1,32,32,128]{4,3,1,0,2:T(8,128)(2,1)}), bf16[2,1,32,32,128]{4,3,1,0,2:T(8,128)(2,1)S(1)}, u32[]{:S(2)}, u32[]{:S(2)}) async-start(bf16[2,1,32,32,128]{4,3,1,0,2:T(8,128)(2,1)} %copy.18), calls=%async_computation.1 | async-start | bytes 1048576 | tf_op jit(solution)/shard_map/all_to_all | solution.py:49
  32.7 3.0 %collective-permute-start.1 = (s32[4,2]{0,1:T(2,128)S(1)}, s32[4,2]{0,1:T(2,128)S(1)}, u32[]{:S(2)}, u32[]{:S(2)}) collective-permute-start(s32[4,2]{0,1:T(2,128)S(1)} %pad_add_fusion), channel_id=1, source_target_pairs={{0,6},{1,7},{2,0},{3,1},{4,2},{5,3},{6,4},{7,5},{8,14},{9,15},{10,... | collective-permute-start | bytes 104 | tf_op jit(solution)/shard_map/ppermute | solution.py:56
  35.7 5.0 %collective-permute-done.1 = s32[4,2]{0,1:T(2,128)S(1)} collective-permute-done((s32[4,2]{0,1:T(2,128)S(1)}, s32[4,2]{0,1:T(2,128)S(1)}, u32[]{:S(2)}, u32[]{:S(2)}) %collective-permute-start.1) | collective-permute-done | bytes 64 | tf_op jit(solution)/shard_map/ppermute | solution.py:56
  40.7 5.1 %collective-permute-start.2 = (s32[8,2]{0,1:T(2,128)S(1)}, s32[8,2]{0,1:T(2,128)S(1)}, u32[]{:S(2)}, u32[]{:S(2)}) collective-permute-start(s32[8,2]{0,1:T(2,128)S(1)} %pad_add_fusion.1), channel_id=1, source_target_pairs={{0,4},{1,5},{2,6},{3,7},{4,0},{5,1},{6,2},{7,3},{8,12},{9,13},{10,... | collective-permute-start | bytes 200 | tf_op jit(solution)/shard_map/ppermute | solution.py:56
  45.8 1.3 collective-permute-done.2
  48.0 2.3 %convolution_bitcast_fusion = f32[2,4,16,32,256]{4,3,1,0,2:T(8,128)S(1)} fusion(f32[1,16,4,32,128]{4,3,2,0,1:T(8,128)S(1)} %bitcast.37, f32[1,16,4,32,128]{4,3,2,0,1:T(8,128)S(1)} %bitcast.36, s32[16,128]{1,0:T(8,128)S(1)} %iota_add_fusion.1), kind=kOutput, calls=%fused_computation | convolution fusion | flops 1611661312 | bytes 6299648 | tf_op jit(solution)/shard_map/qkzab,kby->qzkay/dot_general | solution.py:66
  50.8 3.6 %convolution_bitcast_fusion.1 = f32[2,4,256,256]{2,3,1,0:T(8,128)S(1)} fusion(f32[2,4,512,256]{3,2,1,0:T(8,128)S(1)} %bitcast.33, s32[512]{0:T(512)S(1)} %add.86), kind=kOutput, calls=%fused_computation.6 | convolution fusion | flops 3221356544 | bytes 6293504 | tf_op jit(solution)/shard_map/rx,qzry->qzxy/dot_general | solution.py:74
  54.7 1.3 copy.23
  56.0 1.3 copy.24
  57.4 0.6 dynamic-slice
  58.6 52.8 %all-reduce.6.cloned.1.call-done = (f32[4,256,256]{2,0,1:T(4,128)}, f32[4,256,256]{2,0,1:T(4,128)}) async-done(((f32[4,256,256]{2,0,1:T(4,128)}, f32[4,256,256]{2,0,1:T(4,128)}), (f32[4,256,256]{2,0,1:T(4,128)}, f32[4,256,256]{2,0,1:T(4,128)})) %all-reduce.6.cloned.1.call-update) | async-done | bytes 2097168
  111.4 1.1 fusion.13
  112.6 3.1 %collective-permute-start.3 = (f32[4,1,256]{2,0,1:T(4,128)S(1)}, f32[4,1,256]{2,0,1:T(4,128)S(1)}, u32[]{:S(2)}, u32[]{:S(2)}) collective-permute-start(f32[4,1,256]{2,0,1:T(4,128)S(1)} %get-tuple-element.13), channel_id=1, source_target_pairs={{0,8},{8,16},{16,24},{1,9},{9,17},{17,25},{2,10},{10,18},{18,26},{... | collective-permute-start | bytes 12296 | tf_op jit(solution)/shard_map/ppermute | solution.py:19
  115.6 1.9 %collective-permute-start.4 = (f32[4,1,256]{2,0,1:T(4,128)S(1)}, f32[4,1,256]{2,0,1:T(4,128)S(1)}, u32[]{:S(2)}, u32[]{:S(2)}) collective-permute-start(f32[4,1,256]{2,0,1:T(4,128)S(1)} %get-tuple-element.14), channel_id=1, source_target_pairs={{8,0},{16,8},{24,16},{9,1},{17,9},{25,17},{10,2},{18,10},{26,18},{... | collective-permute-start | bytes 12296 | tf_op jit(solution)/shard_map/ppermute | solution.py:21
  117.6 3.0 %collective-permute-done.4 = f32[4,1,256]{2,0,1:T(4,128)S(1)} collective-permute-done((f32[4,1,256]{2,0,1:T(4,128)S(1)}, f32[4,1,256]{2,0,1:T(4,128)S(1)}, u32[]{:S(2)}, u32[]{:S(2)}) %collective-permute-start.4) | collective-permute-done | bytes 4128 | tf_op jit(solution)/shard_map/ppermute | solution.py:21
  120.7 2.0 %collective-permute-start.5 = (f32[1,66,256]{2,0,1:T(1,128)S(1)}, f32[1,66,256]{2,0,1:T(1,128)S(1)}, u32[]{:S(2)}, u32[]{:S(2)}) collective-permute-start(f32[1,66,256]{2,0,1:T(1,128)S(1)} %get-tuple-element.12), channel_id=1, source_target_pairs={{1,0},{2,1},{3,2},{4,3},{5,4},{6,5},{7,6},{9,8},{10,9},{11,10},{12... | collective-permute-start | bytes 202760 | tf_op jit(solution)/shard_map/ppermute | solution.py:21
  122.7 4.2 %collective-permute-start.6 = (f32[1,66,256]{2,0,1:T(1,128)S(1)}, f32[1,66,256]{2,0,1:T(1,128)S(1)}, u32[]{:S(2)}, u32[]{:S(2)}) collective-permute-start(f32[1,66,256]{2,0,1:T(1,128)S(1)} %get-tuple-element.11), channel_id=1, source_target_pairs={{0,1},{1,2},{2,3},{3,4},{4,5},{5,6},{6,7},{8,9},{9,10},{10,11},{11... | collective-permute-start | bytes 202760 | tf_op jit(solution)/shard_map/ppermute | solution.py:19
  126.9 1.3 collective-permute-done.6
  128.2 0.7 select_maximum_fusion
  129.4 0.8 copy.25
  (30 shorter events, 2.5 us)
Async XLA Ops:
  6.5 7.8 %copy-start.1 = (s32[2,2]{1,0:T(2,128)S(1)}, s32[2,2]{1,0:T(2,128)}, u32[]{:S(2)}) copy-start(s32[2,2]{1,0:T(2,128)} %param.5) | copy-start | bytes 52
  6.5 7.9 %copy-start = (bf16[2,1,32,32,128]{4,3,2,1,0:T(8,128)(2,1)S(1)}, bf16[2,1,32,32,128]{4,3,2,1,0:T(8,128)(2,1)}, u32[]{:S(2)}) copy-start(bf16[2,1,32,32,128]{4,3,2,1,0:T(8,128)(2,1)} %param.4) | copy-start | bytes 1572868
  8.5 19.5 %all-to-all-start = ((bf16[2,1,32,32,128]{4,3,1,0,2:T(8,128)(2,1)}), bf16[2,1,32,32,128]{4,3,1,0,2:T(8,128)(2,1)S(1)}, u32[]{:S(2)}, u32[]{:S(2)}) async-start(bf16[2,1,32,32,128]{4,3,1,0,2:T(8,128)(2,1)} %copy.17), calls=%async_computation | async-start | bytes 1048576 | tf_op jit(solution)/shard_map/all_to_all | solution.py:48
  14.4 18.2 %collective-permute-start = (s32[2,2]{0,1:T(2,128)S(1)}, s32[2,2]{0,1:T(2,128)S(1)}, u32[]{:S(2)}, u32[]{:S(2)}) collective-permute-start(s32[2,2]{0,1:T(2,128)S(1)} %copy.15), channel_id=1, source_target_pairs={{0,7},{1,0},{2,1},{3,2},{4,3},{5,4},{6,5},{7,6},{8,15},{9,8},{10,9... | collective-permute-start | bytes 56 | tf_op jit(solution)/shard_map/ppermute | solution.py:56
  28.1 19.4 %all-to-all-start.1 = ((bf16[2,1,32,32,128]{4,3,1,0,2:T(8,128)(2,1)}), bf16[2,1,32,32,128]{4,3,1,0,2:T(8,128)(2,1)S(1)}, u32[]{:S(2)}, u32[]{:S(2)}) async-start(bf16[2,1,32,32,128]{4,3,1,0,2:T(8,128)(2,1)} %copy.18), calls=%async_computation.1 | async-start | bytes 1048576 | tf_op jit(solution)/shard_map/all_to_all | solution.py:49
  32.6 78.8 %all-reduce.6.cloned.1.call-start = ((), (), s32[]{:S(2)}) async-start(), calls=%async_computation.2 | async-start | bytes 4194304
  32.7 8.0 %collective-permute-start.1 = (s32[4,2]{0,1:T(2,128)S(1)}, s32[4,2]{0,1:T(2,128)S(1)}, u32[]{:S(2)}, u32[]{:S(2)}) collective-permute-start(s32[4,2]{0,1:T(2,128)S(1)} %pad_add_fusion), channel_id=1, source_target_pairs={{0,6},{1,7},{2,0},{3,1},{4,2},{5,3},{6,4},{7,5},{8,14},{9,15},{10,... | collective-permute-start | bytes 104 | tf_op jit(solution)/shard_map/ppermute | solution.py:56
  40.7 6.3 %collective-permute-start.2 = (s32[8,2]{0,1:T(2,128)S(1)}, s32[8,2]{0,1:T(2,128)S(1)}, u32[]{:S(2)}, u32[]{:S(2)}) collective-permute-start(s32[8,2]{0,1:T(2,128)S(1)} %pad_add_fusion.1), channel_id=1, source_target_pairs={{0,4},{1,5},{2,6},{3,7},{4,0},{5,1},{6,2},{7,3},{8,12},{9,13},{10,... | collective-permute-start | bytes 200 | tf_op jit(solution)/shard_map/ppermute | solution.py:56
  56.0 1.3 copy-start.2
  112.6 5.0 %collective-permute-start.3 = (f32[4,1,256]{2,0,1:T(4,128)S(1)}, f32[4,1,256]{2,0,1:T(4,128)S(1)}, u32[]{:S(2)}, u32[]{:S(2)}) collective-permute-start(f32[4,1,256]{2,0,1:T(4,128)S(1)} %get-tuple-element.13), channel_id=1, source_target_pairs={{0,8},{8,16},{16,24},{1,9},{9,17},{17,25},{2,10},{10,18},{18,26},{... | collective-permute-start | bytes 12296 | tf_op jit(solution)/shard_map/ppermute | solution.py:19
  115.6 4.9 %collective-permute-start.4 = (f32[4,1,256]{2,0,1:T(4,128)S(1)}, f32[4,1,256]{2,0,1:T(4,128)S(1)}, u32[]{:S(2)}, u32[]{:S(2)}) collective-permute-start(f32[4,1,256]{2,0,1:T(4,128)S(1)} %get-tuple-element.14), channel_id=1, source_target_pairs={{8,0},{16,8},{24,16},{9,1},{17,9},{25,17},{10,2},{18,10},{26,18},{... | collective-permute-start | bytes 12296 | tf_op jit(solution)/shard_map/ppermute | solution.py:21
  120.7 6.2 %collective-permute-start.5 = (f32[1,66,256]{2,0,1:T(1,128)S(1)}, f32[1,66,256]{2,0,1:T(1,128)S(1)}, u32[]{:S(2)}, u32[]{:S(2)}) collective-permute-start(f32[1,66,256]{2,0,1:T(1,128)S(1)} %get-tuple-element.12), channel_id=1, source_target_pairs={{1,0},{2,1},{3,2},{4,3},{5,4},{6,5},{7,6},{9,8},{10,9},{11,10},{12... | collective-permute-start | bytes 202760 | tf_op jit(solution)/shard_map/ppermute | solution.py:21
  122.7 5.5 %collective-permute-start.6 = (f32[1,66,256]{2,0,1:T(1,128)S(1)}, f32[1,66,256]{2,0,1:T(1,128)S(1)}, u32[]{:S(2)}, u32[]{:S(2)}) collective-permute-start(f32[1,66,256]{2,0,1:T(1,128)S(1)} %get-tuple-element.11), channel_id=1, source_target_pairs={{0,1},{1,2},{2,3},{3,4},{4,5},{5,6},{6,7},{8,9},{9,10},{10,11},{11... | collective-permute-start | bytes 202760 | tf_op jit(solution)/shard_map/ppermute | solution.py:19
Sparse Core Ops, SparseCore 0:
  57.5 53.9 all-reduce.5
